TPU v7x, 32 devices: a whole 2x2x4 slice. The times are simulated.
32 devices in a mesh: groups: 2 (over x), seq: 16 (over z, y, core).
Axes of the slice: x: 2, y: 2, z: 4, core: 2. Of those that a mesh axis runs over, the one named last changes fastest.
Arguments:
- first_queries: bfloat16 [4096, 2048], P(('groups', 'seq')), parts along dimension 0, may hold values from -12 to 12
- second_queries: bfloat16 [4096, 2048], P(('groups', 'seq')), parts along dimension 0, may hold values from -12 to 12
- common_keys: bfloat16 [4096, 512], P(('groups', 'seq')), parts along dimension 0, may hold values from -4 to 4
- common_values: bfloat16 [4096, 512], P(('groups', 'seq')), parts along dimension 0, may hold values from -6 to 6
- lengths: int32 [8], P('groups'), parts along dimension 0, may hold values from 1 to 1024, 2048 in all
Outputs:
- first_output: bfloat16 [4096, 2048], P(('groups', 'seq')), parts along dimension 0
- second_output: bfloat16 [4096, 2048], P(('groups', 'seq')), parts along dimension 0
There are 2 independent parts, one for each index of `groups`. A program takes and returns all parts, laid end to end along the dimension named above; each array names one. Nothing has to cross between parts.
Inputs may be any that keep to these rules, and one draw needn't show every extreme that they name: `lengths`: the 4 documents lie end to end in order and fill all 2048 positions.
All inputs are finite; a program needn't handle non-finite values.
Results may differ from a plain program's by a relative error of at most 0.0034.
Values may be sent and summed in bfloat16 or wider, within the bound.
A program may use at most 64 MiB of HBM per device.

v0:
```python
import functools
import math

import jax
import jax.numpy as jnp
from jax import lax
from jax.experimental import pallas as pl
from jax.experimental.pallas import tpu as pltpu
from jax.sharding import PartitionSpec as P

HEAD_WIDTH = 128
QUERY_HEAD_COUNT = 16
KEY_VALUE_HEADS = 4
SHARE = QUERY_HEAD_COUNT // KEY_VALUE_HEADS
PLANE = 4
CHUNKS = 2
TILE = 256
SUM_ROWS = 16
HIDDEN = -1e30
MESH = pl.DeviceIdType.MESH


def kernel(
    members,
    hops,
    lengths_ref,
    first_ref,
    second_ref,
    keys_ref,
    values_ref,
    first_out,
    second_out,
    key_buffer,
    value_buffer,
    turned,
    bias,
    highest,
    total,
    send_sem,
    recv_sem,
):
    group = lax.axis_index("groups")
    me = lax.axis_index("seq")
    planes = members // PLANE
    plane = me // PLANE
    column = me % PLANE
    base = plane * PLANE
    beside = column + 1 - 2 * (column % 2)
    across = (column + 2) % PLANE
    corner = (beside + 2) % PLANE
    rows = keys_ref.shape[0]
    chunk_width = keys_ref.shape[1] // CHUNKS
    own = (keys_ref, values_ref)
    buffers = (key_buffer, value_buffer)
    has_upper = plane + 1 < planes
    has_lower = plane >= 1

    barrier = pltpu.get_barrier_semaphore()

    def greet(seat):
        pl.semaphore_signal(barrier, inc=1, device_id=(group, seat), device_id_type=MESH)

    greet(base + beside)
    greet(base + across)

    @pl.when(has_upper)
    def _():
        greet(me + PLANE)

    @pl.when(has_lower)
    def _():
        greet(me - PLANE)

    pl.semaphore_wait(barrier, 2 + has_upper.astype(jnp.int32) + has_lower.astype(jnp.int32))

    def wanted(hop, source, target):
        if hop == 0:
            return source < target
        if hop == hops:
            return (source > target) & (plane >= hop)
        return plane >= hop

    def slot(kind, hop, seat, chunk):
        start = pl.multiple_of(((hops - hop) * PLANE + seat) * rows, rows)
        return buffers[kind].at[pl.ds(start, rows), pl.ds(chunk * chunk_width, chunk_width)]

    def held(kind, hop, seat, chunk):
        if hop == 0:
            return own[kind].at[:, pl.ds(chunk * chunk_width, chunk_width)]
        return slot(kind, hop, seat, chunk)

    pending = []

    def send(condition, source, destination, target, index):
        @pl.when(condition)
        def _():
            pltpu.make_async_remote_copy(
                src_ref=source,
                dst_ref=destination,
                send_sem=send_sem.at[index],
                recv_sem=recv_sem.at[index],
                device_id=(group, target),
                device_id_type=MESH,
            ).start()

        pending.append((condition, source, destination, target, index))

    def receive(condition, destination, index):
        @pl.when(condition)
        def _():
            pltpu.make_async_remote_copy(
                src_ref=destination,
                dst_ref=destination,
                send_sem=send_sem.at[index],
                recv_sem=recv_sem.at[index],
                device_id=(group, base + beside),
                device_id_type=MESH,
            ).wait_recv()

    def send_up(hop, chunk, kind):
        send(
            has_upper & (plane >= hop - 1),
            held(kind, hop - 1, column, chunk),
            slot(kind, hop, column, chunk),
            me + PLANE,
            (kind, hop, 0, chunk),
        )

    def send_across(hop, chunk, kind):
        send(
            wanted(hop, column, across),
            held(kind, hop, column, chunk),
            slot(kind, hop, column, chunk),
            base + across,
            (kind, hop, 2, chunk),
        )

    def send_beside(hop, chunk, kind):
        send(
            wanted(hop, column, beside),
            held(kind, hop, column, chunk),
            slot(kind, hop, column, chunk),
            base + beside,
            (kind, hop, 1, chunk),
        )

    def pass_beside(hop, chunk, kind):
        send(
            wanted(hop, across, beside),
            slot(kind, hop, across, chunk),
            slot(kind, hop, across, chunk),
            base + beside,
            (kind, hop, 3, chunk),
        )

    def take_up(hop, chunk, kind):
        receive(plane >= hop, slot(kind, hop, column, chunk), (kind, hop, 0, chunk))

    def take_across(hop, chunk, kind):
        receive(
            wanted(hop, across, column),
            slot(kind, hop, across, chunk),
            (kind, hop, 2, chunk),
        )

    def take_beside(hop, chunk, kind):
        receive(
            wanted(hop, beside, column),
            slot(kind, hop, beside, chunk),
            (kind, hop, 1, chunk),
        )
        receive(
            wanted(hop, corner, column),
            slot(kind, hop, corner, chunk),
            (kind, hop, 3, chunk),
        )

    for chunk in range(CHUNKS):
        for kind in range(2):
            send_up(1, chunk, kind)
            send_across(0, chunk, kind)
            send_beside(0, chunk, kind)

    own_start = pl.multiple_of((hops * PLANE + column) * rows, rows)
    key_buffer[pl.ds(own_start, rows), :] = keys_ref[...]
    value_buffer[pl.ds(own_start, rows), :] = values_ref[...]
    nothing = jnp.zeros(keys_ref.shape, keys_ref.dtype)
    for seat in range(PLANE):

        @pl.when(seat > column)
        def _():
            start = (hops * PLANE + seat) * rows
            key_buffer[pl.ds(start, rows), :] = nothing
            value_buffer[pl.ds(start, rows), :] = nothing

        @pl.when((seat < column) & (plane >= hops))
        def _():
            start = seat * rows
            key_buffer[pl.ds(start, rows), :] = nothing
            value_buffer[pl.ds(start, rows), :] = nothing

    place = lax.broadcasted_iota(jnp.int32, (1, rows), 1) + me * rows
    bound = jnp.int32(0)
    begin = jnp.zeros((1, rows), jnp.int32)
    for document in range(lengths_ref.shape[0] - 1):
        bound = bound + lengths_ref[document]
        begin = jnp.where(place >= bound, bound, begin)
    plane_rows = PLANE * rows
    for hop in range(hops + 1):
        key_place = lax.broadcasted_iota(jnp.int32, (plane_rows, rows), 0) + (
            (plane - hop) * plane_rows
        )
        visible = (key_place >= begin) & (key_place <= place)
        bias[pl.ds((hops - hop) * plane_rows, plane_rows), :] = jnp.where(
            visible, 0.0, HIDDEN
        )

    queries = (first_ref, second_ref)
    outputs = (first_out, second_out)
    stacked = 2 * SHARE * rows

    def turn(head, carry):
        for layer in range(2):
            for member in range(SHARE):
                start = pl.multiple_of((head * SHARE + member) * HEAD_WIDTH, HEAD_WIDTH)
                piece = queries[layer][:, pl.ds(start, HEAD_WIDTH)]
                turned[head, :, pl.ds((layer * SHARE + member) * rows, rows)] = piece.T
        return carry

    lax.fori_loop(0, KEY_VALUE_HEADS, turn, 0)

    factor = HEAD_WIDTH ** (-0.5) * math.log2(math.e)
    heads_per_chunk = KEY_VALUE_HEADS // CHUNKS

    def absorb(first_row, key_rows, fresh, head):
        columns = pl.ds(pl.multiple_of(head * HEAD_WIDTH, HEAD_WIDTH), HEAD_WIDTH)
        tile_keys = key_buffer[pl.ds(first_row, key_rows), columns]
        tile_values = value_buffer[pl.ds(first_row, key_rows), columns]
        flat_values = jnp.concatenate(
            [tile_values.T, jnp.ones((SUM_ROWS, key_rows), tile_values.dtype)], axis=0
        )
        hidden = bias[pl.ds(first_row, key_rows), :]
        hidden = jnp.concatenate([hidden] * (TILE // rows), axis=1)

        def score(start):
            span = pl.ds(start, TILE)
            scores = jnp.dot(tile_keys, turned[head, :, span], preferred_element_type=jnp.float32)
            masked = scores + hidden
            top = jnp.max(masked, axis=0, keepdims=True)
            if not fresh:
                top = jnp.maximum(top, highest[head, :, span])
            return masked, top

        def blend(start, weights, top):
            span = pl.ds(start, TILE)
            product = jnp.dot(flat_values, weights, preferred_element_type=jnp.float32)
            if not fresh:
                before = highest[head, :, span]
                product = product + total[head, :, span] * jnp.exp2((before - top) * factor)
            highest[head, :, span] = top
            total[head, :, span] = product

        starts = list(range(0, stacked, TILE))
        upcoming = score(starts[0])
        earlier = None
        for place_in, start in enumerate(starts):
            masked, top = upcoming
            if place_in + 1 < len(starts):
                upcoming = score(starts[place_in + 1])
            weights = jnp.exp2((masked - top) * factor).astype(jnp.bfloat16)
            if earlier is not None:
                blend(*earlier)
            earlier = (start, weights, top)
        blend(*earlier)

    def attend(hop, chunk):
        first_row = (hops - hop) * plane_rows
        half = plane_rows // 2

        def over(first, count):
            def step(index, carry):
                absorb(first, count, hop == 0, chunk * heads_per_chunk + index)
                return carry

            lax.fori_loop(0, heads_per_chunk, step, 0)

        if hop == 0:

            @pl.when(column < PLANE // 2)
            def _():
                over(first_row, half)

            @pl.when(column >= PLANE // 2)
            def _():
                over(first_row, plane_rows)
        elif hop == hops:

            @pl.when((plane >= hop) & (column < PLANE // 2))
            def _():
                over(first_row, plane_rows)

            @pl.when((plane >= hop) & (column >= PLANE // 2))
            def _():
                over(first_row + half, half)
        else:

            @pl.when(plane >= hop)
            def _():
                over(first_row, plane_rows)

    def finish(chunk):
        def step(index, carry):
            head = chunk * heads_per_chunk + index
            for layer in range(2):
                for member in range(SHARE):
                    span = pl.ds((layer * SHARE + member) * rows, rows)
                    weighted = total[head, 0:HEAD_WIDTH, span]
                    mass = total[head, HEAD_WIDTH : HEAD_WIDTH + 1, span]
                    blended = (weighted / mass).astype(jnp.bfloat16)
                    start = pl.multiple_of((head * SHARE + member) * HEAD_WIDTH, HEAD_WIDTH)
                    outputs[layer][:, pl.ds(start, HEAD_WIDTH)] = blended.T
            return carry

        lax.fori_loop(0, heads_per_chunk, step, 0)

    for hop in range(hops + 1):
        for chunk in range(CHUNKS):
            for kind in range(2):
                if hop < hops:
                    take_up(hop + 1, chunk, kind)
                    if hop + 2 <= hops:
                        send_up(hop + 2, chunk, kind)
                    send_across(hop + 1, chunk, kind)
                    send_beside(hop + 1, chunk, kind)
                take_across(hop, chunk, kind)
                pass_beside(hop, chunk, kind)
            for kind in range(2):
                take_beside(hop, chunk, kind)
            attend(hop, chunk)
            if hop == hops:
                finish(chunk)

    for condition, source, destination, target, index in pending:

        @pl.when(condition)
        def _():
            pltpu.make_async_remote_copy(
                src_ref=source,
                dst_ref=destination,
                send_sem=send_sem.at[index],
                recv_sem=recv_sem.at[index],
                device_id=(group, target),
                device_id_type=MESH,
            ).wait_send()


def on_device(first_queries, second_queries, common_keys, common_values, lengths):
    members = lax.axis_size("seq")
    hops = members // (2 * PLANE)
    rows = common_keys.shape[0]
    slots = (hops + 1) * PLANE
    width = common_keys.shape[1]
    stacked = 2 * SHARE * rows
    in_vmem = pl.BlockSpec(memory_space=pltpu.VMEM)
    shape = jax.ShapeDtypeStruct(first_queries.shape, jnp.bfloat16)
    semaphores = pltpu.SemaphoreType.DMA((2, hops + 1, 4, CHUNKS))
    return pl.pallas_call(
        functools.partial(kernel, members, hops),
        out_shape=(shape, shape),
        in_specs=[pl.BlockSpec(memory_space=pltpu.SMEM)] + [in_vmem] * 4,
        out_specs=(in_vmem, in_vmem),
        scratch_shapes=[
            pltpu.VMEM((slots * rows, width), jnp.bfloat16),
            pltpu.VMEM((slots * rows, width), jnp.bfloat16),
            pltpu.VMEM((KEY_VALUE_HEADS, HEAD_WIDTH, stacked), jnp.bfloat16),
            pltpu.VMEM((slots * rows, rows), jnp.float32),
            pltpu.VMEM((KEY_VALUE_HEADS, 1, stacked), jnp.float32),
            pltpu.VMEM((KEY_VALUE_HEADS, HEAD_WIDTH + SUM_ROWS, stacked), jnp.float32),
            semaphores,
            semaphores,
        ],
        compiler_params=pltpu.CompilerParams(collective_id=0, has_side_effects=True),
    )(lengths, first_queries, second_queries, common_keys, common_values)


def solution(mesh):
    in_specs = (
        P(("groups", "seq"), None),
        P(("groups", "seq"), None),
        P(("groups", "seq"), None),
        P(("groups", "seq"), None),
        P("groups"),
    )
    out_specs = (P(("groups", "seq"), None), P(("groups", "seq"), None))
    return jax.shard_map(
        on_device, mesh=mesh, in_specs=in_specs, out_specs=out_specs, check_vma=False
    )
```

profile of v0, /device:TPU:19, one launch (start us, length us, event | category | flops | bytes accessed | tf_op | source)
XLA Modules:
  0.0 32.2 jit_solution(13500573709043829625)
XLA Ops:
  0.6 28.8 %shard_map.68 = (bf16[128,2048]{1,0:T(8,128)(2,1)}, bf16[128,2048]{1,0:T(8,128)(2,1)}) custom-call(s32[4]{0:T(128)} %lengths_ref.1, bf16[128,2048]{1,0:T(8,128)(2,1)} %first_ref.1, bf16[128,2048]{1,0:T(8,128)(2,1)} %second_ref.1, bf16[128,512]{1,0:T(8,128)(2,1)} %keys_ref.1, bf16[128,512]{1,0:T(8,128)(2,1)} %values_ref.1), custom_call_target="tpu_custom_call" | custom-call | tf_op jit(solution)/shard_map/pallas_call | solution.py:367
  29.4 0.0 copy-start
  29.4 1.9 %copy.9 = bf16[128,2048]{1,0:T(8,128)(2,1)} copy(bf16[128,2048]{1,0:T(8,128)(2,1)} %get-tuple-element.4) | data formatting | bytes 1048576
  31.4 0.0 copy-done
  31.4 0.8 %copy.10 = bf16[128,2048]{1,0:T(8,128)(2,1)} copy(bf16[128,2048]{1,0:T(8,128)(2,1)S(1)} %copy-done) | data formatting | bytes 1048576
Async XLA Ops:
  29.4 2.0 %copy-start = (bf16[128,2048]{1,0:T(8,128)(2,1)S(1)}, bf16[128,2048]{1,0:T(8,128)(2,1)}, u32[]{:S(2)}) copy-start(bf16[128,2048]{1,0:T(8,128)(2,1)} %get-tuple-element.5) | copy-start | bytes 1572868
where the time goes:
time: 32.4 us; the launch traced here: 32.2 us
  Pallas kernels  28.8 us (89%)
  local copies, waits for them, and re-layouts  2.74 us (8%)
  between operations  0.65 us (2%)
    pallas_call x1, Pallas kernels, on_device(): pl.pallas_call(functools.partial(kernel, members, hops), out_shape=(shape...  28.8 us
    unnamed x4, local copies, waits for them, and re-layouts  2.74 us

commit v1 on v0

--- a/solution.py
+++ b/solution.py
@@ -15,12 +15,17 @@
 PLANE = 4
 CHUNKS = 2
 TILE = 256
+CORES = 2
+REACH = 4
+Y_LAG = 3
+Z_PAIR_LAG = 2
+Y_PAIR_LAG = 5
 SUM_ROWS = 16
 HIDDEN = -1e30
 MESH = pl.DeviceIdType.MESH
 
 
-def kernel(
+def wide_kernel(
     members,
     hops,
     lengths_ref,
@@ -354,7 +359,7 @@
             ).wait_send()
 
 
-def on_device(first_queries, second_queries, common_keys, common_values, lengths):
+def on_device_wide(first_queries, second_queries, common_keys, common_values, lengths):
     members = lax.axis_size("seq")
     hops = members // (2 * PLANE)
     rows = common_keys.shape[0]
@@ -365,7 +370,7 @@
     shape = jax.ShapeDtypeStruct(first_queries.shape, jnp.bfloat16)
     semaphores = pltpu.SemaphoreType.DMA((2, hops + 1, 4, CHUNKS))
     return pl.pallas_call(
-        functools.partial(kernel, members, hops),
+        functools.partial(wide_kernel, members, hops),
         out_shape=(shape, shape),
         in_specs=[pl.BlockSpec(memory_space=pltpu.SMEM)] + [in_vmem] * 4,
         out_specs=(in_vmem, in_vmem),
@@ -383,6 +388,388 @@
     )(lengths, first_queries, second_queries, common_keys, common_values)
 
 
+def kernel(
+    planes,
+    lengths_ref,
+    first_ref,
+    second_ref,
+    keys_ref,
+    values_ref,
+    first_out,
+    second_out,
+    queries,
+    held,
+    bias,
+    scores,
+    weights,
+    tops,
+    highest,
+    total,
+    own_sem,
+    query_sem,
+    z_send,
+    z_recv,
+    y_send,
+    y_recv,
+    pair_send,
+    pair_recv,
+):
+    group = lax.axis_index("groups")
+    me = lax.axis_index("seq")
+    plane = me // PLANE
+    column = (me // CORES) % 2
+    core = me % CORES
+    chip = me // CORES
+    partner = me + 1 - 2 * core
+    beside = me + CORES - 2 * CORES * column
+    rows = keys_ref.shape[0]
+    unit = CORES * rows
+    stacked = 2 * SHARE * rows
+    factor = HEAD_WIDTH ** (-0.5) * math.log2(math.e)
+    has_upper = plane + 1 < planes
+    items = 4 * KEY_VALUE_HEADS
+
+    def slot(kind, head, distance):
+        start = pl.multiple_of(distance * unit + core * rows, rows)
+        return held.at[kind, head, pl.ds(start, rows), :]
+
+    def parts_of(item):
+        return item // (2 * KEY_VALUE_HEADS), (item // KEY_VALUE_HEADS) % 2, item % KEY_VALUE_HEADS
+
+    def own_copy(kind, head):
+        return pltpu.make_async_copy(
+            (keys_ref, values_ref)[kind].at[:, pl.ds(head * HEAD_WIDTH, HEAD_WIDTH)],
+            slot(kind, head, 0),
+            own_sem.at[kind, head],
+        )
+
+    def query_copy(layer, head):
+        start = pl.multiple_of(head * HEAD_WIDTH, HEAD_WIDTH)
+        first = pl.multiple_of((layer * SHARE + head % SHARE) * rows, rows)
+        return pltpu.make_async_copy(
+            (first_ref, second_ref)[layer].at[:, pl.ds(start, HEAD_WIDTH)],
+            queries.at[head // SHARE, pl.ds(first, rows), :],
+            query_sem.at[layer, head],
+        )
+
+    barrier = pltpu.get_barrier_semaphore()
+
+    def greet(seat):
+        pl.semaphore_signal(barrier, inc=1, device_id=(group, seat), device_id_type=MESH)
+
+    @pl.when(plane >= 1)
+    def _():
+        greet(me - PLANE)
+
+    @pl.when(plane >= 1 - column)
+    def _():
+        greet(beside)
+
+    greet(partner)
+
+    for head in range(KEY_VALUE_HEADS):
+        own_copy(0, head).start()
+    for head in range(KEY_VALUE_HEADS):
+        own_copy(1, head).start()
+
+    def load_queries(head, carry):
+        for layer in range(2):
+            query_copy(layer, head).start()
+        return carry
+
+    lax.fori_loop(0, QUERY_HEAD_COUNT, load_queries, 0)
+
+    def remote(source, target_slot, send_sem, recv_sem, seat):
+        return pltpu.make_async_remote_copy(
+            src_ref=source,
+            dst_ref=target_slot,
+            send_sem=send_sem,
+            recv_sem=recv_sem,
+            device_id=(group, seat),
+            device_id_type=MESH,
+        )
+
+    def z_copy(item):
+        kind, hop, head = parts_of(item)
+        return remote(
+            slot(kind, head, 2 * hop),
+            slot(kind, head, 2 * hop + 2),
+            z_send.at[item],
+            z_recv.at[item],
+            me + PLANE,
+        )
+
+    def y_copy(item):
+        kind, half, head = parts_of(item)
+        return remote(
+            slot(kind, head, 2 * half + 2 * column),
+            slot(kind, head, 2 * half + 1),
+            y_send.at[item],
+            y_recv.at[item],
+            beside,
+        )
+
+    def pair_copy(kind, distance, head):
+        place = slot(kind, head, distance)
+        index = (kind, distance, head)
+        return remote(place, place, pair_send.at[index], pair_recv.at[index], partner)
+
+    def y_sends(half):
+        return plane >= half + column
+
+    def y_takes(half):
+        return plane >= half + 1 - column
+
+    def start_own(kind):
+        @pl.when(has_upper)
+        def _():
+            for head in range(KEY_VALUE_HEADS):
+                z_copy(kind * 2 * KEY_VALUE_HEADS + head).start()
+
+        @pl.when(column == 0)
+        def _():
+            for head in range(KEY_VALUE_HEADS):
+                y_copy(kind * 2 * KEY_VALUE_HEADS + head).start()
+
+    pl.semaphore_wait(
+        barrier, 1 + has_upper.astype(jnp.int32) + (plane >= column).astype(jnp.int32)
+    )
+    for head in range(KEY_VALUE_HEADS):
+        own_copy(0, head).wait()
+    start_own(0)
+    for head in range(KEY_VALUE_HEADS):
+        pair_copy(0, 0, head).start()
+    for head in range(KEY_VALUE_HEADS):
+        own_copy(1, head).wait()
+    for head in range(KEY_VALUE_HEADS):
+        pair_copy(1, 0, head).start()
+
+    @pl.when(plane == 0)
+    def _():
+        start_own(1)
+
+    place = lax.broadcasted_iota(jnp.int32, (rows, unit), 0) + me * rows
+    bound = jnp.int32(0)
+    begin = jnp.zeros((rows, unit), jnp.int32)
+    for document in range(lengths_ref.shape[0] - 1):
+        bound = bound + lengths_ref[document]
+        begin = jnp.where(place >= bound, bound, begin)
+    for distance in range(REACH + 1):
+        key_place = lax.broadcasted_iota(jnp.int32, (rows, unit), 1) + (chip - distance) * unit
+        visible = (key_place >= begin) & (key_place <= place)
+        bias[distance] = jnp.where(visible, 0.0, HIDDEN)
+
+    def unit_rows(distance):
+        return pl.ds(pl.multiple_of(distance * unit, unit), unit)
+
+    def weigh(head, distance, fresh, room):
+        keys = held[0, head, unit_rows(distance), :]
+        half = stacked // 2
+        for first in range(0, stacked, half):
+            scores[room, pl.ds(first, half), :] = lax.dot_general(
+                queries[head, pl.ds(first, half), :],
+                keys,
+                (((1,), (1,)), ((), ())),
+                preferred_element_type=jnp.float32,
+            )
+        step = rows // 2
+        for first in range(0, stacked, step):
+            span = pl.ds(first, step)
+            masked = scores[room, span, :] + bias[distance, pl.ds(first % rows, step), :]
+            top = jnp.max(masked, axis=1, keepdims=True)
+            weights[head, distance, span, :] = jnp.exp2((masked - top) * factor).astype(
+                jnp.bfloat16
+            )
+            spread = jnp.broadcast_to(top, (step, HEAD_WIDTH))
+            tops[head, distance, span, :] = spread
+            if fresh:
+                highest[head, span, :] = spread
+            else:
+                highest[head, span, :] = jnp.maximum(highest[head, span, :], spread)
+
+    def blend(head, distance, fresh):
+        values = held[1, head, unit_rows(distance), :]
+        product = jnp.dot(
+            weights[head, distance],
+            jnp.concatenate([values, jnp.ones_like(values)], axis=1),
+            preferred_element_type=jnp.float32,
+        )
+        step = rows // 2
+        for first in range(0, stacked, step):
+            span = pl.ds(first, step)
+            share = jnp.exp2((tops[head, distance, span, :] - highest[head, span, :]) * factor)
+            part = product[first : first + step] * jnp.concatenate([share, share], axis=1)
+            if fresh:
+                total[head, span, :] = part
+            else:
+                total[head, span, :] = total[head, span, :] + part
+
+    outputs = (first_out, second_out)
+
+    def finish(head):
+        for layer in range(2):
+            for member in range(SHARE):
+                span = pl.ds((layer * SHARE + member) * rows, rows)
+                blended = total[head, span, 0:HEAD_WIDTH] / total[head, span, HEAD_WIDTH:]
+                start = pl.multiple_of((head * SHARE + member) * HEAD_WIDTH, HEAD_WIDTH)
+                outputs[layer][:, pl.ds(start, HEAD_WIDTH)] = blended.astype(jnp.bfloat16)
+
+    def wait_queries(head, carry):
+        for layer in range(2):
+            query_copy(layer, head).wait()
+        return carry
+
+    lax.fori_loop(0, QUERY_HEAD_COUNT, wait_queries, 0)
+
+    def nearest(head, carry):
+        pair_copy(0, 0, head).wait_recv()
+        weigh(head, 0, True, 0)
+        return carry
+
+    lax.fori_loop(0, KEY_VALUE_HEADS, nearest, 0)
+
+    y_last = items - 1 + Y_PAIR_LAG
+    settle = 2 * KEY_VALUE_HEADS - KEY_VALUE_HEADS + Y_PAIR_LAG
+
+    def step(index, carry):
+        kind, hop, head = parts_of(index)
+
+        @pl.when((index < items) & (plane >= hop + 1))
+        def _():
+            z_copy(index).wait_recv()
+
+            @pl.when(column == 1)
+            def _():
+                y_copy(index).start()
+
+            @pl.when((column == 0) & (hop == 0))
+            def _():
+                y_copy(index + KEY_VALUE_HEADS).start()
+
+            @pl.when(has_upper & (hop == 0))
+            def _():
+                z_copy(index + KEY_VALUE_HEADS).start()
+
+            pair_copy(kind, 2 * hop + 2, head).start()
+
+        @pl.when((index == KEY_VALUE_HEADS - 1) & (plane >= 1))
+        def _():
+            start_own(1)
+
+        y_item = index - Y_LAG
+        y_kind, y_half, y_head = parts_of(y_item)
+
+        @pl.when((y_item >= 0) & (y_item < items) & y_takes(y_half))
+        def _():
+            y_copy(y_item).wait_recv()
+            pair_copy(y_kind, 2 * y_half + 1, y_head).start()
+
+        pair_item = index - Z_PAIR_LAG
+        pair_kind, pair_hop, pair_head = parts_of(pair_item)
+
+        @pl.when((pair_item >= 0) & (pair_item < items) & (plane >= pair_hop + 1))
+        def _():
+            distance = 2 * pair_hop + 2
+            pair_copy(pair_kind, distance, pair_head).wait_recv()
+
+            @pl.when(pair_kind == 0)
+            def _():
+                weigh(pair_head, distance, False, 0)
+
+            @pl.when(pair_kind == 1)
+            def _():
+                blend(pair_head, distance, False)
+
+        late_item = index - Y_PAIR_LAG
+        late_kind, late_half, late_head = parts_of(late_item)
+
+        @pl.when((late_item >= 0) & y_takes(late_half))
+        def _():
+            distance = 2 * late_half + 1
+            pair_copy(late_kind, distance, late_head).wait_recv()
+
+            @pl.when(late_kind == 0)
+            def _():
+                weigh(late_head, distance, False, 1)
+
+            @pl.when(late_kind == 1)
+            def _():
+                blend(late_head, distance, False)
+
+        @pl.when((index >= settle) & (index < settle + KEY_VALUE_HEADS))
+        def _():
+            pair_copy(1, 0, index - settle).wait_recv()
+            blend(index - settle, 0, True)
+
+        @pl.when(index >= y_last + 1 - KEY_VALUE_HEADS)
+        def _():
+            finish(index - (y_last + 1 - KEY_VALUE_HEADS))
+
+        return carry
+
+    lax.fori_loop(0, y_last + 1, step, 0)
+
+    def settle_sends(item, carry):
+        kind, hop, head = parts_of(item)
+
+        @pl.when(has_upper & (plane >= hop))
+        def _():
+            z_copy(item).wait_send()
+
+        @pl.when(y_sends(hop))
+        def _():
+            y_copy(item).wait_send()
+
+        return carry
+
+    lax.fori_loop(0, items, settle_sends, 0)
+    for distance in range(REACH + 1):
+
+        @pl.when(chip >= distance)
+        def _():
+            for kind in range(2):
+                for head in range(KEY_VALUE_HEADS):
+                    pair_copy(kind, distance, head).wait_send()
+
+
+def on_device(first_queries, second_queries, common_keys, common_values, lengths):
+    planes = lax.axis_size("seq") // PLANE
+    rows = common_keys.shape[0]
+    unit = CORES * rows
+    units = REACH + 1
+    stacked = 2 * SHARE * rows
+    in_vmem = pl.BlockSpec(memory_space=pltpu.VMEM)
+    anywhere = pl.BlockSpec(memory_space=pl.ANY)
+    shape = jax.ShapeDtypeStruct(first_queries.shape, jnp.bfloat16)
+    link_sems = pltpu.SemaphoreType.DMA((4 * KEY_VALUE_HEADS,))
+    pair_sems = pltpu.SemaphoreType.DMA((2, units, KEY_VALUE_HEADS))
+    return pl.pallas_call(
+        functools.partial(kernel, planes),
+        out_shape=(shape, shape),
+        in_specs=[pl.BlockSpec(memory_space=pltpu.SMEM)] + [anywhere] * 4,
+        out_specs=(in_vmem, in_vmem),
+        scratch_shapes=[
+            pltpu.VMEM((KEY_VALUE_HEADS, stacked, HEAD_WIDTH), jnp.bfloat16),
+            pltpu.VMEM((2, KEY_VALUE_HEADS, units * unit, HEAD_WIDTH), jnp.bfloat16),
+            pltpu.VMEM((units, rows, unit), jnp.float32),
+            pltpu.VMEM((2, stacked, unit), jnp.float32),
+            pltpu.VMEM((KEY_VALUE_HEADS, units, stacked, unit), jnp.bfloat16),
+            pltpu.VMEM((KEY_VALUE_HEADS, units, stacked, HEAD_WIDTH), jnp.float32),
+            pltpu.VMEM((KEY_VALUE_HEADS, stacked, HEAD_WIDTH), jnp.float32),
+            pltpu.VMEM((KEY_VALUE_HEADS, stacked, 2 * HEAD_WIDTH), jnp.float32),
+            pltpu.SemaphoreType.DMA((2, KEY_VALUE_HEADS)),
+            pltpu.SemaphoreType.DMA((2, QUERY_HEAD_COUNT)),
+            link_sems,
+            link_sems,
+            link_sems,
+            link_sems,
+            pair_sems,
+            pair_sems,
+        ],
+        compiler_params=pltpu.CompilerParams(collective_id=0, has_side_effects=True),
+    )(lengths, first_queries, second_queries, common_keys, common_values)
+
+
 def solution(mesh):
     in_specs = (
         P(("groups", "seq"), None),
@@ -392,6 +779,7 @@
         P("groups"),
     )
     out_specs = (P(("groups", "seq"), None), P(("groups", "seq"), None))
+    body = on_device if mesh.shape["seq"] == 2 * REACH * CORES else on_device_wide
     return jax.shard_map(
-        on_device, mesh=mesh, in_specs=in_specs, out_specs=out_specs, check_vma=False
+        body, mesh=mesh, in_specs=in_specs, out_specs=out_specs, check_vma=False
     )

time: 32.4 us -> 31 us (0.957)
  Pallas kernels: 28.8 us -> 27.4 us
    pallas_call x1, Pallas kernels: 28.8 us -> 27.4 us  [on_device(): pl.pallas_call(functools.partial(kernel, planes), out_shape=(shape, shape...]
where the time goes in v1:
time: 31 us; the launch traced here: 30.8 us
  Pallas kernels  27.4 us (88%)
  local copies, waits for them, and re-layouts  2.74 us (9%)
  between operations  0.65 us (2%)
    pallas_call x1, Pallas kernels, on_device(): pl.pallas_call(functools.partial(kernel, planes), out_shape=(shape, shape...  27.4 us
    unnamed x4, local copies, waits for them, and re-layouts  2.74 us

profile of v1, /device:TPU:19, one launch (start us, length us, event | category | flops | bytes accessed | tf_op | source)
XLA Modules:
  0.0 30.8 jit_solution(10959051405990748246)
XLA Ops:
  0.6 27.4 %shard_map.68 = (bf16[128,2048]{1,0:T(8,128)(2,1)}, bf16[128,2048]{1,0:T(8,128)(2,1)}) custom-call(s32[4]{0:T(128)} %lengths_ref.1, bf16[128,2048]{1,0:T(8,128)(2,1)} %first_ref.1, bf16[128,2048]{1,0:T(8,128)(2,1)} %second_ref.1, bf16[128,512]{1,0:T(8,128)(2,1)} %keys_ref.1, bf16[128,512]{1,0:T(8,128)(2,1)} %values_ref.1), custom_call_target="tpu_custom_call" | custom-call | tf_op jit(solution)/shard_map/pallas_call | solution.py:746
  28.0 0.0 copy-start
  28.0 1.9 %copy.9 = bf16[128,2048]{1,0:T(8,128)(2,1)} copy(bf16[128,2048]{1,0:T(8,128)(2,1)} %get-tuple-element.4) | data formatting | bytes 1048576
  30.0 0.0 copy-done
  30.0 0.8 %copy.10 = bf16[128,2048]{1,0:T(8,128)(2,1)} copy(bf16[128,2048]{1,0:T(8,128)(2,1)S(1)} %copy-done) | data formatting | bytes 1048576
Async XLA Ops:
  28.0 2.0 %copy-start = (bf16[128,2048]{1,0:T(8,128)(2,1)S(1)}, bf16[128,2048]{1,0:T(8,128)(2,1)}, u32[]{:S(2)}) copy-start(bf16[128,2048]{1,0:T(8,128)(2,1)} %get-tuple-element.5) | copy-start | bytes 1572868

commit v2 on v1

--- a/solution.py
+++ b/solution.py
@@ -17,9 +17,13 @@
 TILE = 256
 CORES = 2
 REACH = 4
-Y_LAG = 3
+DISTANCES = (0, 2, 1, 4, 3)
+TEAMS = ((0, 2), (2, 2), (4, 1))
+Y_LAG = 5
 Z_PAIR_LAG = 2
-Y_PAIR_LAG = 5
+Y_PAIR_LAG = 7
+WEIGH_STEPS = (2, 7, 11)
+BLEND_STEPS = (12, 15, 19)
 SUM_ROWS = 16
 HIDDEN = -1e30
 MESH = pl.DeviceIdType.MESH
@@ -429,8 +433,8 @@
     has_upper = plane + 1 < planes
     items = 4 * KEY_VALUE_HEADS
 
-    def slot(kind, head, distance):
-        start = pl.multiple_of(distance * unit + core * rows, rows)
+    def slot(kind, head, position):
+        start = pl.multiple_of(position * unit + core * rows, rows)
         return held.at[kind, head, pl.ds(start, rows), :]
 
     def parts_of(item):
@@ -440,7 +444,7 @@
         return pltpu.make_async_copy(
             (keys_ref, values_ref)[kind].at[:, pl.ds(head * HEAD_WIDTH, HEAD_WIDTH)],
             slot(kind, head, 0),
-            own_sem.at[kind, head],
+            own_sem.at[kind],
         )
 
     def query_copy(layer, head):
@@ -449,7 +453,7 @@
         return pltpu.make_async_copy(
             (first_ref, second_ref)[layer].at[:, pl.ds(start, HEAD_WIDTH)],
             queries.at[head // SHARE, pl.ds(first, rows), :],
-            query_sem.at[layer, head],
+            query_sem,
         )
 
     barrier = pltpu.get_barrier_semaphore()
@@ -492,9 +496,9 @@
     def z_copy(item):
         kind, hop, head = parts_of(item)
         return remote(
-            slot(kind, head, 2 * hop),
-            slot(kind, head, 2 * hop + 2),
-            z_send.at[item],
+            slot(kind, head, hop),
+            slot(kind, head, 2 * hop + 1),
+            z_send.at[hop],
             z_recv.at[item],
             me + PLANE,
         )
@@ -502,17 +506,25 @@
     def y_copy(item):
         kind, half, head = parts_of(item)
         return remote(
-            slot(kind, head, 2 * half + 2 * column),
-            slot(kind, head, 2 * half + 1),
-            y_send.at[item],
+            slot(kind, head, half + column * (half + 1)),
+            slot(kind, head, 2 * half + 2),
+            y_send.at[half],
             y_recv.at[item],
             beside,
         )
 
-    def pair_copy(kind, distance, head):
-        place = slot(kind, head, distance)
-        index = (kind, distance, head)
-        return remote(place, place, pair_send.at[index], pair_recv.at[index], partner)
+    def pair_copy(kind, position, head):
+        place = slot(kind, head, position)
+        index = (kind, position, head)
+        return remote(place, place, pair_send.at[position], pair_recv.at[index], partner)
+
+    def all_sent(sem):
+        every = held.at[:, :, pl.ds(0, rows), :]
+        remote(every, every, sem, sem, partner).wait_send()
+
+    def own_arrived(kind):
+        every = held.at[kind, :, pl.ds(pl.multiple_of(core * rows, rows), rows), :]
+        pltpu.make_async_copy(every, every, own_sem.at[kind]).wait()
 
     def y_sends(half):
         return plane >= half + column
@@ -534,13 +546,11 @@
     pl.semaphore_wait(
         barrier, 1 + has_upper.astype(jnp.int32) + (plane >= column).astype(jnp.int32)
     )
-    for head in range(KEY_VALUE_HEADS):
-        own_copy(0, head).wait()
+    own_arrived(0)
     start_own(0)
     for head in range(KEY_VALUE_HEADS):
         pair_copy(0, 0, head).start()
-    for head in range(KEY_VALUE_HEADS):
-        own_copy(1, head).wait()
+    own_arrived(1)
     for head in range(KEY_VALUE_HEADS):
         pair_copy(1, 0, head).start()
 
@@ -554,52 +564,56 @@
     for document in range(lengths_ref.shape[0] - 1):
         bound = bound + lengths_ref[document]
         begin = jnp.where(place >= bound, bound, begin)
-    for distance in range(REACH + 1):
+    nothing = jnp.zeros((2, KEY_VALUE_HEADS, unit, HEAD_WIDTH), held.dtype)
+    for position, distance in enumerate(DISTANCES):
+        spot = pl.ds(position * unit, unit)
         key_place = lax.broadcasted_iota(jnp.int32, (rows, unit), 1) + (chip - distance) * unit
         visible = (key_place >= begin) & (key_place <= place)
-        bias[distance] = jnp.where(visible, 0.0, HIDDEN)
-
-    def unit_rows(distance):
-        return pl.ds(pl.multiple_of(distance * unit, unit), unit)
-
-    def weigh(head, distance, fresh, room):
-        keys = held[0, head, unit_rows(distance), :]
+        bias[:, spot] = jnp.where(visible, 0.0, HIDDEN)
+
+        @pl.when(chip < distance)
+        def _():
+            held[:, :, spot, :] = nothing
+
+    def weigh(head, team):
+        spot = pl.ds(TEAMS[team][0] * unit, TEAMS[team][1] * unit)
+        width = TEAMS[team][1] * unit
+        keys = held[0, head, spot, :]
         half = stacked // 2
         for first in range(0, stacked, half):
-            scores[room, pl.ds(first, half), :] = lax.dot_general(
+            scores[pl.ds(first, half), 0:width] = lax.dot_general(
                 queries[head, pl.ds(first, half), :],
                 keys,
                 (((1,), (1,)), ((), ())),
                 preferred_element_type=jnp.float32,
             )
+        step = rows // 4
+        for first in range(0, stacked, step):
+            span = pl.ds(first, step)
+            masked = scores[span, 0:width] + bias[pl.ds(first % rows, step), spot]
+            top = jnp.max(masked, axis=1, keepdims=True)
+            weights[head, span, spot] = jnp.exp2((masked - top) * factor).astype(jnp.bfloat16)
+            spread = jnp.broadcast_to(top, (step, HEAD_WIDTH))
+            tops[head, team, span, :] = spread
+            if team == 0:
+                highest[head, span, :] = spread
+            else:
+                highest[head, span, :] = jnp.maximum(highest[head, span, :], spread)
+
+    def blend(head, team):
+        spot = pl.ds(TEAMS[team][0] * unit, TEAMS[team][1] * unit)
+        values = held[1, head, spot, :]
+        product = jnp.dot(
+            weights[head, :, spot],
+            jnp.concatenate([values, jnp.ones_like(values)], axis=1),
+            preferred_element_type=jnp.float32,
+        )
         step = rows // 2
         for first in range(0, stacked, step):
             span = pl.ds(first, step)
-            masked = scores[room, span, :] + bias[distance, pl.ds(first % rows, step), :]
-            top = jnp.max(masked, axis=1, keepdims=True)
-            weights[head, distance, span, :] = jnp.exp2((masked - top) * factor).astype(
-                jnp.bfloat16
-            )
-            spread = jnp.broadcast_to(top, (step, HEAD_WIDTH))
-            tops[head, distance, span, :] = spread
-            if fresh:
-                highest[head, span, :] = spread
-            else:
-                highest[head, span, :] = jnp.maximum(highest[head, span, :], spread)
-
-    def blend(head, distance, fresh):
-        values = held[1, head, unit_rows(distance), :]
-        product = jnp.dot(
-            weights[head, distance],
-            jnp.concatenate([values, jnp.ones_like(values)], axis=1),
-            preferred_element_type=jnp.float32,
-        )
-        step = rows // 2
-        for first in range(0, stacked, step):
-            span = pl.ds(first, step)
-            share = jnp.exp2((tops[head, distance, span, :] - highest[head, span, :]) * factor)
+            share = jnp.exp2((tops[head, team, span, :] - highest[head, span, :]) * factor)
             part = product[first : first + step] * jnp.concatenate([share, share], axis=1)
-            if fresh:
+            if team == 0:
                 total[head, span, :] = part
             else:
                 total[head, span, :] = total[head, span, :] + part
@@ -614,22 +628,24 @@
                 start = pl.multiple_of((head * SHARE + member) * HEAD_WIDTH, HEAD_WIDTH)
                 outputs[layer][:, pl.ds(start, HEAD_WIDTH)] = blended.astype(jnp.bfloat16)
 
-    def wait_queries(head, carry):
-        for layer in range(2):
-            query_copy(layer, head).wait()
-        return carry
-
-    lax.fori_loop(0, QUERY_HEAD_COUNT, wait_queries, 0)
-
-    def nearest(head, carry):
-        pair_copy(0, 0, head).wait_recv()
-        weigh(head, 0, True, 0)
-        return carry
-
-    lax.fori_loop(0, KEY_VALUE_HEADS, nearest, 0)
-
-    y_last = items - 1 + Y_PAIR_LAG
-    settle = 2 * KEY_VALUE_HEADS - KEY_VALUE_HEADS + Y_PAIR_LAG
+    pltpu.make_async_copy(queries, queries, query_sem).wait()
+
+    def at(index, begin, stages):
+        return (index >= begin) & (index < begin + stages)
+
+    def z_ready(item):
+        kind, hop, head = parts_of(item)
+
+        @pl.when((item >= 0) & (item < items) & (plane >= hop + 1))
+        def _():
+            pair_copy(kind, 2 * hop + 1, head).wait_recv()
+
+    def y_ready(item):
+        kind, half, head = parts_of(item)
+
+        @pl.when((item >= 0) & (item < items) & y_takes(half))
+        def _():
+            pair_copy(kind, 2 * half + 2, head).wait_recv()
 
     def step(index, carry):
         kind, hop, head = parts_of(index)
@@ -650,7 +666,7 @@
             def _():
                 z_copy(index + KEY_VALUE_HEADS).start()
 
-            pair_copy(kind, 2 * hop + 2, head).start()
+            pair_copy(kind, 2 * hop + 1, head).start()
 
         @pl.when((index == KEY_VALUE_HEADS - 1) & (plane >= 1))
         def _():
@@ -662,74 +678,43 @@
         @pl.when((y_item >= 0) & (y_item < items) & y_takes(y_half))
         def _():
             y_copy(y_item).wait_recv()
-            pair_copy(y_kind, 2 * y_half + 1, y_head).start()
-
-        pair_item = index - Z_PAIR_LAG
-        pair_kind, pair_hop, pair_head = parts_of(pair_item)
-
-        @pl.when((pair_item >= 0) & (pair_item < items) & (plane >= pair_hop + 1))
-        def _():
-            distance = 2 * pair_hop + 2
-            pair_copy(pair_kind, distance, pair_head).wait_recv()
-
-            @pl.when(pair_kind == 0)
-            def _():
-                weigh(pair_head, distance, False, 0)
-
-            @pl.when(pair_kind == 1)
-            def _():
-                blend(pair_head, distance, False)
-
-        late_item = index - Y_PAIR_LAG
-        late_kind, late_half, late_head = parts_of(late_item)
-
-        @pl.when((late_item >= 0) & y_takes(late_half))
-        def _():
-            distance = 2 * late_half + 1
-            pair_copy(late_kind, distance, late_head).wait_recv()
-
-            @pl.when(late_kind == 0)
-            def _():
-                weigh(late_head, distance, False, 1)
-
-            @pl.when(late_kind == 1)
-            def _():
-                blend(late_head, distance, False)
-
-        @pl.when((index >= settle) & (index < settle + KEY_VALUE_HEADS))
-        def _():
-            pair_copy(1, 0, index - settle).wait_recv()
-            blend(index - settle, 0, True)
-
-        @pl.when(index >= y_last + 1 - KEY_VALUE_HEADS)
-        def _():
-            finish(index - (y_last + 1 - KEY_VALUE_HEADS))
+            pair_copy(y_kind, 2 * y_half + 2, y_head).start()
+
+        z_ready(index - Z_PAIR_LAG)
+        y_ready(index - Y_PAIR_LAG)
+
+        for kind_done, stages in ((0, WEIGH_STEPS), (1, BLEND_STEPS)):
+            for team, begin in enumerate(stages):
+
+                @pl.when(at(index, begin, KEY_VALUE_HEADS))
+                def _():
+                    if team == 0:
+                        pair_copy(kind_done, 0, index - begin).wait_recv()
+                    (weigh, blend)[kind_done](index - begin, team)
+
+        @pl.when(at(index, BLEND_STEPS[-1], KEY_VALUE_HEADS))
+        def _():
+            finish(index - BLEND_STEPS[-1])
 
         return carry
 
-    lax.fori_loop(0, y_last + 1, step, 0)
-
-    def settle_sends(item, carry):
-        kind, hop, head = parts_of(item)
+    lax.fori_loop(0, BLEND_STEPS[-1] + KEY_VALUE_HEADS, step, 0)
+
+    for hop in range(2):
 
         @pl.when(has_upper & (plane >= hop))
         def _():
-            z_copy(item).wait_send()
+            all_sent(z_send.at[hop])
 
         @pl.when(y_sends(hop))
         def _():
-            y_copy(item).wait_send()
-
-        return carry
-
-    lax.fori_loop(0, items, settle_sends, 0)
-    for distance in range(REACH + 1):
+            all_sent(y_send.at[hop])
+
+    for position, distance in enumerate(DISTANCES):
 
         @pl.when(chip >= distance)
         def _():
-            for kind in range(2):
-                for head in range(KEY_VALUE_HEADS):
-                    pair_copy(kind, distance, head).wait_send()
+            all_sent(pair_send.at[position])
 
 
 def on_device(first_queries, second_queries, common_keys, common_values, lengths):
@@ -740,10 +725,8 @@
     stacked = 2 * SHARE * rows
     in_vmem = pl.BlockSpec(memory_space=pltpu.VMEM)
     anywhere = pl.BlockSpec(memory_space=pl.ANY)
-    shape = jax.ShapeDtypeStruct(first_queries.shape, jnp.bfloat16)
-    link_sems = pltpu.SemaphoreType.DMA((4 * KEY_VALUE_HEADS,))
-    pair_sems = pltpu.SemaphoreType.DMA((2, units, KEY_VALUE_HEADS))
-    return pl.pallas_call(
+    shape = pltpu.VMEM(first_queries.shape, jnp.bfloat16)
+    placed = pl.pallas_call(
         functools.partial(kernel, planes),
         out_shape=(shape, shape),
         in_specs=[pl.BlockSpec(memory_space=pltpu.SMEM)] + [anywhere] * 4,
@@ -751,23 +734,53 @@
         scratch_shapes=[
             pltpu.VMEM((KEY_VALUE_HEADS, stacked, HEAD_WIDTH), jnp.bfloat16),
             pltpu.VMEM((2, KEY_VALUE_HEADS, units * unit, HEAD_WIDTH), jnp.bfloat16),
-            pltpu.VMEM((units, rows, unit), jnp.float32),
-            pltpu.VMEM((2, stacked, unit), jnp.float32),
-            pltpu.VMEM((KEY_VALUE_HEADS, units, stacked, unit), jnp.bfloat16),
-            pltpu.VMEM((KEY_VALUE_HEADS, units, stacked, HEAD_WIDTH), jnp.float32),
+            pltpu.VMEM((rows, units * unit), jnp.float32),
+            pltpu.VMEM((stacked, 2 * unit), jnp.float32),
+            pltpu.VMEM((KEY_VALUE_HEADS, stacked, units * unit), jnp.bfloat16),
+            pltpu.VMEM((KEY_VALUE_HEADS, len(TEAMS), stacked, HEAD_WIDTH), jnp.float32),
             pltpu.VMEM((KEY_VALUE_HEADS, stacked, HEAD_WIDTH), jnp.float32),
             pltpu.VMEM((KEY_VALUE_HEADS, stacked, 2 * HEAD_WIDTH), jnp.float32),
-            pltpu.SemaphoreType.DMA((2, KEY_VALUE_HEADS)),
-            pltpu.SemaphoreType.DMA((2, QUERY_HEAD_COUNT)),
-            link_sems,
-            link_sems,
-            link_sems,
-            link_sems,
-            pair_sems,
-            pair_sems,
+            pltpu.SemaphoreType.DMA((2,)),
+            pltpu.SemaphoreType.DMA,
+            pltpu.SemaphoreType.DMA((2,)),
+            pltpu.SemaphoreType.DMA((4 * KEY_VALUE_HEADS,)),
+            pltpu.SemaphoreType.DMA((2,)),
+            pltpu.SemaphoreType.DMA((4 * KEY_VALUE_HEADS,)),
+            pltpu.SemaphoreType.DMA((units,)),
+            pltpu.SemaphoreType.DMA((2, units, KEY_VALUE_HEADS)),
         ],
         compiler_params=pltpu.CompilerParams(collective_id=0, has_side_effects=True),
     )(lengths, first_queries, second_queries, common_keys, common_values)
+    return to_memory(*placed)
+
+
+def place_outputs(first_ref, second_ref, first_out, second_out, sems):
+    copies = [
+        pltpu.make_async_copy(source, target, sems.at[index])
+        for index, (source, target) in enumerate(
+            ((first_ref, first_out), (second_ref, second_out))
+        )
+    ]
+    for copy in copies:
+        copy.start()
+    for copy in copies:
+        copy.wait()
+
+
+def to_memory(first, second):
+    in_vmem = pl.BlockSpec(memory_space=pltpu.VMEM)
+    anywhere = pl.BlockSpec(memory_space=pltpu.HBM)
+    shape = jax.ShapeDtypeStruct(first.shape, first.dtype)
+    return pl.pallas_call(
+        place_outputs,
+        out_shape=(shape, shape),
+        in_specs=[in_vmem] * 2,
+        out_specs=(anywhere, anywhere),
+        scratch_shapes=[pltpu.SemaphoreType.DMA((2,))],
+    )(
+        pltpu.with_memory_space_constraint(first, pltpu.VMEM),
+        pltpu.with_memory_space_constraint(second, pltpu.VMEM),
+    )
 
 
 def solution(mesh):

time: 31 us -> 24.6 us (0.79)
  Pallas kernels: 27.4 us -> 23.8 us
  local copies, waits for them, and re-layouts: 2.74 us -> 0 us
    pallas_call x1, Pallas kernels: 27.4 us -> 22.8 us  [on_device(): pl.pallas_call(functools.partial(kernel, planes), out_shape=(shape, shape...]
    unnamed x4 -> x0, local copies, waits for them, and re-layouts: 2.74 us -> none
    pallas_call x0 -> x1, Pallas kernels: none -> 0.99 us  [to_memory(): pl.pallas_call(place_outputs, out_shape=(shape, shape), in_specs=[in_vmem...]
where the time goes in v2:
time: 24.6 us; the launch traced here: 24.4 us
  Pallas kernels  23.8 us (97%)
  between operations  0.64 us (3%)
    pallas_call x1, Pallas kernels, on_device(): pl.pallas_call(functools.partial(kernel, planes), out_shape=(shape, shape...  22.8 us
    pallas_call x1, Pallas kernels, to_memory(): pl.pallas_call(place_outputs, out_shape=(shape, shape), in_specs=[in_vmem...  0.99 us

profile of v2, /device:TPU:19, one launch (start us, length us, event | category | flops | bytes accessed | tf_op | source)
XLA Modules:
  0.0 24.4 jit_solution(8388345644454130565)
XLA Ops:
  0.6 22.8 %shard_map.68 = (bf16[128,2048]{1,0:T(8,128)(2,1)S(1)}, bf16[128,2048]{1,0:T(8,128)(2,1)S(1)}) custom-call(s32[4]{0:T(128)} %lengths_ref.1, bf16[128,2048]{1,0:T(8,128)(2,1)} %first_ref.1, bf16[128,2048]{1,0:T(8,128)(2,1)} %second_ref.1, bf16[128,512]{1,0:T(8,128)(2,1)} %keys_ref.1, bf16[128,512]{1,0:T(8,128)(2,1)} %values_ref.1), custom_call_target="tpu_custom_call" | custom-call | tf_op jit(solution)/shard_map/pallas_call | solution.py:729
  23.4 1.0 %shard_map.69 = (bf16[128,2048]{1,0:T(8,128)(2,1)}, bf16[128,2048]{1,0:T(8,128)(2,1)}) custom-call(bf16[128,2048]{1,0:T(8,128)(2,1)S(1)} %get-tuple-element.4.first_ref, bf16[128,2048]{1,0:T(8,128)(2,1)S(1)} %get-tuple-element.5.second_ref), custom_call_target="tpu_custom_call" | custom-call | tf_op jit(solution)/shard_map/pallas_call | solution.py:774

commit v3 on v2

--- a/solution.py
+++ b/solution.py
@@ -19,11 +19,12 @@
 REACH = 4
 DISTANCES = (0, 2, 1, 4, 3)
 TEAMS = ((0, 2), (2, 2), (4, 1))
-Y_LAG = 5
-Z_PAIR_LAG = 2
-Y_PAIR_LAG = 7
-WEIGH_STEPS = (2, 7, 11)
-BLEND_STEPS = (12, 15, 19)
+BATCH = 2
+Y_LAG = 2
+Z_PAIR_LAG = 1
+Y_PAIR_LAG = 3
+WEIGH_STEPS = (1, 3, 5)
+BLEND_STEPS = (5, 7, 9)
 SUM_ROWS = 16
 HIDDEN = -1e30
 MESH = pl.DeviceIdType.MESH
@@ -394,7 +395,7 @@
 
 def kernel(
     planes,
-    lengths_ref,
+    lengths_hbm,
     first_ref,
     second_ref,
     keys_ref,
@@ -409,6 +410,8 @@
     tops,
     highest,
     total,
+    lengths_ref,
+    length_sem,
     own_sem,
     query_sem,
     z_send,
@@ -473,6 +476,8 @@
 
     for head in range(KEY_VALUE_HEADS):
         own_copy(0, head).start()
+    length_copy = pltpu.make_async_copy(lengths_hbm, lengths_ref, length_sem)
+    length_copy.start()
     for head in range(KEY_VALUE_HEADS):
         own_copy(1, head).start()
 
@@ -513,9 +518,10 @@
             beside,
         )
 
-    def pair_copy(kind, position, head):
-        place = slot(kind, head, position)
-        index = (kind, position, head)
+    def pair_copy(kind, position, batch, heads):
+        start = pl.multiple_of(position * unit + core * rows, rows)
+        place = held.at[kind, pl.ds(batch * heads, heads), pl.ds(start, rows), :]
+        index = (kind, position, batch)
         return remote(place, place, pair_send.at[position], pair_recv.at[index], partner)
 
     def all_sent(sem):
@@ -548,16 +554,15 @@
     )
     own_arrived(0)
     start_own(0)
-    for head in range(KEY_VALUE_HEADS):
-        pair_copy(0, 0, head).start()
+    pair_copy(0, 0, 0, KEY_VALUE_HEADS).start()
     own_arrived(1)
-    for head in range(KEY_VALUE_HEADS):
-        pair_copy(1, 0, head).start()
+    pair_copy(1, 0, 0, KEY_VALUE_HEADS).start()
 
     @pl.when(plane == 0)
     def _():
         start_own(1)
 
+    length_copy.wait()
     place = lax.broadcasted_iota(jnp.int32, (rows, unit), 0) + me * rows
     bound = jnp.int32(0)
     begin = jnp.zeros((rows, unit), jnp.int32)
@@ -575,13 +580,13 @@
         def _():
             held[:, :, spot, :] = nothing
 
-    def weigh(head, team):
+    def weigh(head, team, room):
         spot = pl.ds(TEAMS[team][0] * unit, TEAMS[team][1] * unit)
         width = TEAMS[team][1] * unit
         keys = held[0, head, spot, :]
         half = stacked // 2
         for first in range(0, stacked, half):
-            scores[pl.ds(first, half), 0:width] = lax.dot_general(
+            scores[room, pl.ds(first, half), 0:width] = lax.dot_general(
                 queries[head, pl.ds(first, half), :],
                 keys,
                 (((1,), (1,)), ((), ())),
@@ -590,7 +595,7 @@
         step = rows // 4
         for first in range(0, stacked, step):
             span = pl.ds(first, step)
-            masked = scores[span, 0:width] + bias[pl.ds(first % rows, step), spot]
+            masked = scores[room, span, 0:width] + bias[pl.ds(first % rows, step), spot]
             top = jnp.max(masked, axis=1, keepdims=True)
             weights[head, span, spot] = jnp.exp2((masked - top) * factor).astype(jnp.bfloat16)
             spread = jnp.broadcast_to(top, (step, HEAD_WIDTH))
@@ -630,75 +635,87 @@
 
     pltpu.make_async_copy(queries, queries, query_sem).wait()
 
-    def at(index, begin, stages):
-        return (index >= begin) & (index < begin + stages)
+    batches = KEY_VALUE_HEADS // BATCH
+    pair_items = 4 * batches
+
+    def batch_parts(item):
+        return item // (2 * batches), (item // batches) % 2, item % batches
 
     def z_ready(item):
-        kind, hop, head = parts_of(item)
-
-        @pl.when((item >= 0) & (item < items) & (plane >= hop + 1))
-        def _():
-            pair_copy(kind, 2 * hop + 1, head).wait_recv()
+        kind, hop, batch = batch_parts(item)
+
+        @pl.when((item >= 0) & (item < pair_items) & (plane >= hop + 1))
+        def _():
+            pair_copy(kind, 2 * hop + 1, batch, BATCH).wait_recv()
 
     def y_ready(item):
-        kind, half, head = parts_of(item)
-
-        @pl.when((item >= 0) & (item < items) & y_takes(half))
-        def _():
-            pair_copy(kind, 2 * half + 2, head).wait_recv()
+        kind, half, batch = batch_parts(item)
+
+        @pl.when((item >= 0) & (item < pair_items) & y_takes(half))
+        def _():
+            pair_copy(kind, 2 * half + 2, batch, BATCH).wait_recv()
+
+    def z_arrival(item):
+        kind, hop, batch = batch_parts(item)
+
+        @pl.when((item < pair_items) & (plane >= hop + 1))
+        def _():
+            for piece in range(BATCH):
+                chunk = item * BATCH + piece
+                z_copy(chunk).wait_recv()
+
+                @pl.when((column == 1) | (hop == 0))
+                def _():
+                    y_copy(chunk + KEY_VALUE_HEADS * (1 - column)).start()
+
+                @pl.when(has_upper & (hop == 0))
+                def _():
+                    z_copy(chunk + KEY_VALUE_HEADS).start()
+
+            pair_copy(kind, 2 * hop + 1, batch, BATCH).start()
+
+        @pl.when((item == batches - 1) & (plane >= 1))
+        def _():
+            start_own(1)
+
+    def y_arrival(item):
+        kind, half, batch = batch_parts(item)
+
+        @pl.when((item >= 0) & (item < pair_items) & y_takes(half))
+        def _():
+            for piece in range(BATCH):
+                y_copy(item * BATCH + piece).wait_recv()
+            pair_copy(kind, 2 * half + 2, batch, BATCH).start()
 
     def step(index, carry):
-        kind, hop, head = parts_of(index)
-
-        @pl.when((index < items) & (plane >= hop + 1))
-        def _():
-            z_copy(index).wait_recv()
-
-            @pl.when(column == 1)
-            def _():
-                y_copy(index).start()
-
-            @pl.when((column == 0) & (hop == 0))
-            def _():
-                y_copy(index + KEY_VALUE_HEADS).start()
-
-            @pl.when(has_upper & (hop == 0))
-            def _():
-                z_copy(index + KEY_VALUE_HEADS).start()
-
-            pair_copy(kind, 2 * hop + 1, head).start()
-
-        @pl.when((index == KEY_VALUE_HEADS - 1) & (plane >= 1))
-        def _():
-            start_own(1)
-
-        y_item = index - Y_LAG
-        y_kind, y_half, y_head = parts_of(y_item)
-
-        @pl.when((y_item >= 0) & (y_item < items) & y_takes(y_half))
-        def _():
-            y_copy(y_item).wait_recv()
-            pair_copy(y_kind, 2 * y_half + 2, y_head).start()
-
+        z_arrival(index)
+        y_arrival(index - Y_LAG)
         z_ready(index - Z_PAIR_LAG)
         y_ready(index - Y_PAIR_LAG)
-
-        for kind_done, stages in ((0, WEIGH_STEPS), (1, BLEND_STEPS)):
+        for kind, stages in ((0, WEIGH_STEPS), (1, BLEND_STEPS)):
             for team, begin in enumerate(stages):
 
-                @pl.when(at(index, begin, KEY_VALUE_HEADS))
+                @pl.when((index >= begin) & (index < begin + batches))
                 def _():
                     if team == 0:
-                        pair_copy(kind_done, 0, index - begin).wait_recv()
-                    (weigh, blend)[kind_done](index - begin, team)
-
-        @pl.when(at(index, BLEND_STEPS[-1], KEY_VALUE_HEADS))
-        def _():
-            finish(index - BLEND_STEPS[-1])
+
+                        @pl.when(index == begin)
+                        def _():
+                            pair_copy(kind, 0, 0, KEY_VALUE_HEADS).wait_recv()
+
+                    for piece in range(BATCH):
+                        head = (index - begin) * BATCH + piece
+                        if kind == 0:
+                            weigh(head, team, piece)
+                        else:
+                            blend(head, team)
+                    if kind == 1 and team == len(TEAMS) - 1:
+                        for piece in range(BATCH):
+                            finish((index - begin) * BATCH + piece)
 
         return carry
 
-    lax.fori_loop(0, BLEND_STEPS[-1] + KEY_VALUE_HEADS, step, 0)
+    lax.fori_loop(0, BLEND_STEPS[-1] + batches, step, 0)
 
     for hop in range(2):
 
@@ -729,17 +746,19 @@
     placed = pl.pallas_call(
         functools.partial(kernel, planes),
         out_shape=(shape, shape),
-        in_specs=[pl.BlockSpec(memory_space=pltpu.SMEM)] + [anywhere] * 4,
+        in_specs=[anywhere] * 5,
         out_specs=(in_vmem, in_vmem),
         scratch_shapes=[
             pltpu.VMEM((KEY_VALUE_HEADS, stacked, HEAD_WIDTH), jnp.bfloat16),
             pltpu.VMEM((2, KEY_VALUE_HEADS, units * unit, HEAD_WIDTH), jnp.bfloat16),
             pltpu.VMEM((rows, units * unit), jnp.float32),
-            pltpu.VMEM((stacked, 2 * unit), jnp.float32),
+            pltpu.VMEM((BATCH, stacked, 2 * unit), jnp.float32),
             pltpu.VMEM((KEY_VALUE_HEADS, stacked, units * unit), jnp.bfloat16),
             pltpu.VMEM((KEY_VALUE_HEADS, len(TEAMS), stacked, HEAD_WIDTH), jnp.float32),
             pltpu.VMEM((KEY_VALUE_HEADS, stacked, HEAD_WIDTH), jnp.float32),
             pltpu.VMEM((KEY_VALUE_HEADS, stacked, 2 * HEAD_WIDTH), jnp.float32),
+            pltpu.SMEM(lengths.shape, lengths.dtype),
+            pltpu.SemaphoreType.DMA,
             pltpu.SemaphoreType.DMA((2,)),
             pltpu.SemaphoreType.DMA,
             pltpu.SemaphoreType.DMA((2,)),
@@ -747,7 +766,7 @@
             pltpu.SemaphoreType.DMA((2,)),
             pltpu.SemaphoreType.DMA((4 * KEY_VALUE_HEADS,)),
             pltpu.SemaphoreType.DMA((units,)),
-            pltpu.SemaphoreType.DMA((2, units, KEY_VALUE_HEADS)),
+            pltpu.SemaphoreType.DMA((2, units, KEY_VALUE_HEADS // BATCH)),
         ],
         compiler_params=pltpu.CompilerParams(collective_id=0, has_side_effects=True),
     )(lengths, first_queries, second_queries, common_keys, common_values)

time: 24.6 us -> 23.2 us (0.943)
  Pallas kernels: 23.8 us -> 22.3 us
    pallas_call x1, Pallas kernels: 22.8 us -> 21.3 us  [on_device(): pl.pallas_call(functools.partial(kernel, planes), out_shape=(shape, shape...]
where the time goes in v3:
time: 23.2 us; the launch traced here: 23 us
  Pallas kernels  22.3 us (96%)
  between operations  0.64 us (3%)
    pallas_call x1, Pallas kernels, on_device(): pl.pallas_call(functools.partial(kernel, planes), out_shape=(shape, shape...  21.3 us
    pallas_call x1, Pallas kernels, to_memory(): pl.pallas_call(place_outputs, out_shape=(shape, shape), in_specs=[in_vmem...  0.99 us

profile of v3, /device:TPU:19, one launch (start us, length us, event | category | flops | bytes accessed | tf_op | source)
XLA Modules:
  0.0 23.0 jit_solution(17746860406747091526)
XLA Ops:
  0.6 21.3 %shard_map.68 = (bf16[128,2048]{1,0:T(8,128)(2,1)S(1)}, bf16[128,2048]{1,0:T(8,128)(2,1)S(1)}) custom-call(s32[4]{0:T(128)} %lengths_hbm.1, bf16[128,2048]{1,0:T(8,128)(2,1)} %first_ref.1, bf16[128,2048]{1,0:T(8,128)(2,1)} %second_ref.1, bf16[128,512]{1,0:T(8,128)(2,1)} %keys_ref.1, bf16[128,512]{1,0:T(8,128)(2,1)} %values_ref.1), custom_call_target="tpu_custom_call" | custom-call | tf_op jit(solution)/shard_map/pallas_call | solution.py:746
  22.0 1.0 %shard_map.69 = (bf16[128,2048]{1,0:T(8,128)(2,1)}, bf16[128,2048]{1,0:T(8,128)(2,1)}) custom-call(bf16[128,2048]{1,0:T(8,128)(2,1)S(1)} %get-tuple-element.4.first_ref, bf16[128,2048]{1,0:T(8,128)(2,1)S(1)} %get-tuple-element.5.second_ref), custom_call_target="tpu_custom_call" | custom-call | tf_op jit(solution)/shard_map/pallas_call | solution.py:793
